TPU v7x, 256 devices: a whole 4x4x8 slice. The times are simulated.
256 devices in a mesh: slab: 128 (over z, y, x), feat: 2 (over core).
Axes of the slice: x: 4, y: 4, z: 8, core: 2. Of those that a mesh axis runs over, the one named last changes fastest.
Arguments:
- states: float32 [40, 65536], P(None, ('slab', 'feat')), may hold values from -6 to 6
- inputs: float32 [65536], P(('slab', 'feat')), may hold values from -4 to 4
- targets: float32 [40, 65536], P(None, ('slab', 'feat')), may hold values from -4 to 4
Outputs:
- local_operators: float32 [128, 40, 862], P('slab', 'feat')
- scaled_duals: float32 [128, 40, 862], P('slab', 'feat')
- consensus: float32 [40, 862], P('feat')
- residual_history: float32 [2, 2], replicated
All inputs are finite; a program needn't handle non-finite values.
Results may differ from a plain program's by a relative error of at most 0.0003.
Values sent between devices are 32-bit elements; how exact they have to be, the bound alone decides.
A program may use at most 64 MiB of HBM per device.

v0:
```python
import jax
import jax.numpy as jnp
from jax import lax
from jax.sharding import Mesh
from jax.sharding import PartitionSpec as P

ITERS = 2
SLAB = ("slab_0", "slab_1", "slab_2")
SLAB_FEAT = ("slab_0", "slab_1", "slab_2", "feat")
penalty = 1.0


def total_of_pieces(array, axis):
    tiles = lax.all_gather(array, axis)
    return tiles.sum(axis=0)


def rows_first(arrays, axis, dims):
    turned = [jnp.moveaxis(a, dim, 0) for a, dim in zip(arrays, dims)]
    widths = [t[0].size for t in turned]
    both = jnp.concatenate([t.reshape(-1, w) for t, w in zip(turned, widths)], axis=1)
    whole = lax.all_gather(both, axis, axis=0, tiled=True)
    tiles = jnp.split(whole, [sum(widths[:k]) for k in range(1, len(widths))], axis=1)
    return tuple(
        (
            jnp.moveaxis(b.reshape(-1, *t.shape[1:]), 0, dim)
            for b, t, dim in zip(tiles, turned, dims)
        )
    )


def by_axis(array, axes):
    for axis in axes:
        array = lax.psum(array, axis)
    return array


def features(states, inputs):
    reduced = states.shape[0]
    blocks = [states]
    for column in range(reduced):
        blocks.append(states[column : column + 1] * states[column:])
    blocks.append(inputs[None, :])
    blocks.append(jnp.ones_like(inputs)[None, :])
    return jnp.concatenate(blocks, 0)


def product(left, right):
    return jnp.dot(left, right, precision=lax.Precision.HIGHEST, preferred_element_type=jnp.float32)


def solve_rows(factor, right_side):
    return jax.scipy.linalg.cho_solve((factor, True), right_side.T).T


def slab_average(summand):
    return total_of_pieces(summand, SLAB)


def shards(states, inputs, targets):
    reduced = states.shape[0]
    feat_count = lax.axis_size("feat")
    slab_count = lax.axis_size(SLAB)
    half_rows = reduced // feat_count
    all_states, all_targets, all_inputs = rows_first((states, targets, inputs), "feat", (1, 1, 0))
    design = features(all_states, all_inputs)
    row_total = design.shape[1]
    gram_matrix = product(design, design.T) / row_total
    first_row = lax.axis_index("feat") * half_rows
    picked = lax.dynamic_slice_in_dim(all_targets, first_row, half_rows, 0)
    cross = product(picked, design.T) / row_total
    width = gram_matrix.shape[0]
    factor = jnp.linalg.cholesky(gram_matrix + penalty * jnp.eye(width, dtype=jnp.float32))
    consensus = jnp.zeros((half_rows, width), jnp.float32)
    duals = jnp.zeros((half_rows, width), jnp.float32)
    operator_rows = duals
    primal_list = []
    dual_list = []
    for sweep in range(ITERS):
        operator_rows = solve_rows(factor, cross + penalty * (consensus - duals))
        updated = slab_average(operator_rows + duals) / slab_count
        duals = duals + operator_rows - updated
        primal_part = jnp.sum(jnp.square(operator_rows - updated))
        dual_part = penalty * penalty * jnp.sum(jnp.square(updated - consensus))
        primal_sum, dual_sum = (by_axis(primal_part, SLAB_FEAT), by_axis(dual_part, SLAB_FEAT))
        primal_list.append(primal_sum)
        dual_list.append(dual_sum)
        consensus = updated
    history = jnp.stack([jnp.stack(primal_list), jnp.stack(dual_list)])
    residual_history = jnp.sqrt(history / (slab_count * reduced * width))
    return (operator_rows[None], duals[None], consensus, residual_history)


def solution(mesh):
    split = Mesh(
        mesh.devices.reshape(8, 4, 4, mesh.shape["feat"]), ("slab_0", "slab_1", "slab_2", "feat")
    )
    return jax.shard_map(
        shards,
        mesh=split,
        in_specs=(P(None, SLAB_FEAT), P(SLAB_FEAT), P(None, SLAB_FEAT)),
        out_specs=(P(SLAB, "feat", None), P(SLAB, "feat", None), P("feat", None), P()),
        check_vma=False,
    )
```

profile of v0, /device:TPU:1, one launch (start us, length us, event | category | flops | bytes accessed | tf_op | source)
XLA Modules:
  0.0 660.4 jit_solution(3695795320718135102)
XLA Ops:
  8.6 4.8 all_gather.15
  24.2 13.3 %concatenate.49 = f32[862,512]{1,0:T(8,128)S(1)} concatenate(f32[40,512]{1,0:T(8,128)S(1)} %get-tuple-element.61, f32[40,512]{1,0:T(8,128)S(1)} %broadcast_multiply_fusion.1, f32[39,512]{1,0:T(8,128)S(1)} %slice_multiply_fusion.6, f32[38,512]{1,0:T(8,128)S(1)} %slice_multiply_fusion.5, f32[37,512]{1,0:T(8,128)S(1)} %slice_multiply_fusion.4, f32[36,512]{1,0:T(8,128)S(1)} %slice_multiply_fusion.3, ...), dimensions={0} | concatenate | bytes 3530752 | tf_op jit(solution)/shard_map/concatenate | solution.py:45
  37.5 7.8 %convert_add_fusion = (f32[862,862]{0,1:T(8,128)}, f32[862,862]{0,1:T(8,128)}) fusion(f32[862,512]{1,0:T(8,128)S(1)} %concatenate.49), kind=kOutput, calls=%fused_computation.8 | convolution fusion | flops 4568234496 | bytes 7709728 | tf_op jit(solution)/shard_map/dot_general | solution.py:49
  45.4 3.6 copy.12
  52.9 11.7 %cholesky.196 = f32[128,128]{1,0:T(8,128)S(1)} custom-call(f32[128,128]{1,0:T(8,128)S(1)} %cholesky.508), custom_call_target="Cholesky" | custom-call | tf_op jit(solution)/shard_map/jit(cholesky)/cholesky | solution.py:73
  64.7 9.8 %custom-call.56 = f32[1,128,128]{1,2,0:T(8,128)S(1)} custom-call(f32[1,128,128]{2,1,0:T(8,128)S(1)} %get-tuple-element.118), custom_call_target="InvertDiagBlocksLowerTriangular" | custom-call | tf_op jit(solution)/shard_map/jit(cholesky)/cholesky | solution.py:73
  78.2 13.2 %cholesky.217 = f32[128,128]{1,0:T(8,128)} custom-call(f32[128,128]{1,0:T(8,128)} %cholesky.512), custom_call_target="Cholesky" | custom-call | tf_op jit(solution)/shard_map/jit(cholesky)/cholesky | solution.py:73
  92.9 11.7 %custom-call.57 = f32[1,128,128]{1,2,0:T(8,128)} custom-call(f32[1,128,128]{2,1,0:T(8,128)} %get-tuple-element.115), custom_call_target="InvertDiagBlocksLowerTriangular" | custom-call | tf_op jit(solution)/shard_map/jit(cholesky)/cholesky | solution.py:73
  107.4 12.3 %cholesky.413 = f32[128,128]{1,0:T(8,128)} custom-call(f32[128,128]{1,0:T(8,128)S(1)} %cholesky.517), custom_call_target="Cholesky" | custom-call | tf_op jit(solution)/shard_map/jit(cholesky)/cholesky | solution.py:73
  121.4 10.4 %custom-call.58 = f32[1,128,128]{1,2,0:T(8,128)} custom-call(f32[1,128,128]{2,1,0:T(8,128)S(1)} %get-tuple-element.112), custom_call_target="InvertDiagBlocksLowerTriangular" | custom-call | tf_op jit(solution)/shard_map/jit(cholesky)/cholesky | solution.py:73
  134.7 11.9 %cholesky.432 = f32[128,128]{1,0:T(8,128)S(1)} custom-call(f32[128,128]{1,0:T(8,128)S(1)} %cholesky.522), custom_call_target="Cholesky" | custom-call | tf_op jit(solution)/shard_map/jit(cholesky)/cholesky | solution.py:73
  147.3 9.8 %custom-call.59 = f32[1,128,128]{1,2,0:T(8,128)S(1)} custom-call(f32[1,128,128]{2,1,0:T(8,128)S(1)} %get-tuple-element.109), custom_call_target="InvertDiagBlocksLowerTriangular" | custom-call | tf_op jit(solution)/shard_map/jit(cholesky)/cholesky | solution.py:73
  159.1 11.7 %cholesky.451 = f32[128,128]{1,0:T(8,128)S(1)} custom-call(f32[128,128]{1,0:T(8,128)S(1)} %cholesky.527), custom_call_target="Cholesky" | custom-call | tf_op jit(solution)/shard_map/jit(cholesky)/cholesky | solution.py:73
  171.6 9.8 %custom-call.60 = f32[1,128,128]{1,2,0:T(8,128)S(1)} custom-call(f32[1,128,128]{2,1,0:T(8,128)S(1)} %get-tuple-element.106), custom_call_target="InvertDiagBlocksLowerTriangular" | custom-call | tf_op jit(solution)/shard_map/jit(cholesky)/cholesky | solution.py:73
  183.2 11.9 %cholesky.471 = f32[128,128]{1,0:T(8,128)S(1)} custom-call(f32[128,128]{1,0:T(8,128)S(1)} %cholesky.532), custom_call_target="Cholesky" | custom-call | tf_op jit(solution)/shard_map/jit(cholesky)/cholesky | solution.py:73
  195.8 9.8 %custom-call.61 = f32[1,128,128]{1,2,0:T(8,128)S(1)} custom-call(f32[1,128,128]{2,1,0:T(8,128)S(1)} %get-tuple-element.103), custom_call_target="InvertDiagBlocksLowerTriangular" | custom-call | tf_op jit(solution)/shard_map/jit(cholesky)/cholesky | solution.py:73
  207.0 8.6 %cholesky.492 = f32[94,94]{1,0:T(8,128)S(1)} custom-call(f32[94,94]{1,0:T(8,128)S(1)} %convolution_subtract_fusion.5), custom_call_target="Cholesky" | custom-call | tf_op jit(solution)/shard_map/jit(cholesky)/cholesky | solution.py:73
  223.3 18.0 %while.4 = (s32[]{:T(128)}, f32[862,862]{1,0:T(8,128)}, s32[6,2]{0,1:T(2,128)S(1)}, f32[6,128,128]{2,1,0:T(8,128)S(1)}, s32[]{:T(128)}) while((s32[]{:T(128)}, f32[862,862]{1,0:T(8,128)}, s32[6,2]{0,1:T(2,128)S(1)}, f32[6,128,128]{2,1,0:T(8,128)S(1)}, s32[]{:T(128)}) %tuple.121), condition=%wide.while_cond.clone, body=%wide.while_body.clone.sunk | while | flops 2 | bytes 131189 | solution.py:53
  224.0 2.3 bitcast_dynamic-update-slice_fusion.2
  227.0 2.3 bitcast_dynamic-update-slice_fusion.2
  230.0 2.3 bitcast_dynamic-update-slice_fusion.2
  233.0 2.3 bitcast_dynamic-update-slice_fusion.2
  243.2 69.8 %custom-call.64 = f32[7,128,128]{1,2,0:T(8,128)S(1)} custom-call(f32[7,128,128]{2,1,0:T(8,128)} %pad_maximum_fusion), custom_call_target="InvertDiagBlocksLowerTriangular" | custom-call | tf_op jit(solution)/shard_map/jit(_cho_solve)/triangular_solve | solution.py:53
  313.1 3.1 convolution_multiply_fusion
  327.0 131.4 %all-gather.7.cloned.1.call-done = f32[128,20,862]{2,1,0:T(8,128)} async-done(((f32[1,20,862]{2,1,0:T(8,128)}), f32[128,20,862]{2,1,0:T(8,128)}) %all-gather.7.cloned.1.call-update) | async-done | bytes 8826896 | tf_op jit(solution)/shard_map/all_gather | solution.py:14
  458.4 5.4 reduce_sum.54
  473.7 127.5 %all-gather.9.cloned.1.call-done = f32[128,20,862]{2,1,0:T(8,128)} async-done(((f32[1,20,862]{2,1,0:T(8,128)}), f32[128,20,862]{2,1,0:T(8,128)}) %all-gather.9.cloned.1.call-update) | async-done | bytes 8826896 | tf_op jit(solution)/shard_map/all_gather | solution.py:14
  601.2 4.8 reduce_sum.55
  609.2 12.5 %all-reduce.3 = (f32[]{:T(128)}, f32[]{:T(128)}, f32[]{:T(128)}, f32[]{:T(128)}) all-reduce(f32[]{:T(128)} %get-tuple-element.31, f32[]{:T(128)} %get-tuple-element.30, f32[]{:T(128)} %get-tuple-element.32, f32[]{:T(128)} %get-tuple-element.29), channel_id=1, replica_groups=mesh['slab_0'=8,'slab_1'=4,'slab_2'=4,'feat'=2] {'slab_0'}, use_global_device_ids=true, to_apply=%region_32.34 | all-reduce | flops 4 | bytes 32 | tf_op jit(solution)/shard_map/psum | solution.py:34
  621.7 9.1 %all-reduce.5 = (f32[]{:T(128)}, f32[]{:T(128)}, f32[]{:T(128)}, f32[]{:T(128)}) all-reduce(f32[]{:T(128)} %get-tuple-element.41, f32[]{:T(128)} %get-tuple-element.42, f32[]{:T(128)} %get-tuple-element.43, f32[]{:T(128)} %get-tuple-element.44), channel_id=1, replica_groups=mesh['slab_0'=8,'slab_1'=4,'slab_2'=4,'feat'=2] {'slab_1'}, use_global_device_ids=true, to_apply=%region_33.35 | all-reduce | flops 4 | bytes 32 | tf_op jit(solution)/shard_map/psum | solution.py:34
  630.8 7.2 %all-reduce.4 = (f32[]{:T(128)}, f32[]{:T(128)}, f32[]{:T(128)}, f32[]{:T(128)}) all-reduce(f32[]{:T(128)} %get-tuple-element.49, f32[]{:T(128)} %get-tuple-element.50, f32[]{:T(128)} %get-tuple-element.51, f32[]{:T(128)} %get-tuple-element.52), channel_id=1, replica_groups=mesh['slab_0'=8,'slab_1'=4,'slab_2'=4,'feat'=2] {'slab_2'}, use_global_device_ids=true, to_apply=%region_34.36 | all-reduce | flops 4 | bytes 32 | tf_op jit(solution)/shard_map/psum | solution.py:34
  638.0 11.9 %all-reduce.6 = (f32[1]{0:T(128)}, f32[1]{0:T(128)}, f32[1]{0:T(128)}, f32[1]{0:T(128)}) all-reduce(f32[1]{0:T(128)} %bitcast.84, f32[1]{0:T(128)} %bitcast.83, f32[1]{0:T(128)} %bitcast.81, f32[1]{0:T(128)} %bitcast.80), channel_id=1, replica_groups=mesh['slab_0'=8,'slab_1'=4,'slab_2'=4,'feat'=2] {'feat'}, use_global_device_ids=true, to_apply=%region_35.37 | all-reduce | flops 4 | bytes 32 | tf_op jit(solution)/shard_map/psum | solution.py:34
  (217 shorter events, 76.2 us)
Async XLA Ops:
  7.2 451.2 %all-gather.7.cloned.1.call-start = ((), (), s32[]{:S(2)}) async-start(), calls=%async_computation | async-start | bytes 11096064 | tf_op jit(solution)/shard_map/all_gather | solution.py:14
  37.5 7.8 %copy-start = (f32[862,512]{1,0:T(8,128)}, f32[862,512]{1,0:T(8,128)S(1)}, u32[]{:S(2)}) copy-start(f32[862,512]{1,0:T(8,128)S(1)} %concatenate.49) | copy-start | bytes 5296132
  51.3 1.6 copy-start.3
  221.4 0.9 copy-start.9
  221.4 1.9 copy-start.7
  221.7 1.7 copy-start.1
  241.4 75.0 %copy-start.2 = (f32[862,862]{1,0:T(8,128)S(1)}, f32[862,862]{1,0:T(8,128)}, u32[]{:S(2)}) copy-start(f32[862,862]{1,0:T(8,128)} %get-tuple-element.215) | copy-start | bytes 8916532
  316.1 10.8 %copy-start.6 = (f32[862,20]{0,1:T(8,128)}, f32[862,20]{0,1:T(8,128)S(1)}, u32[]{:S(2)}) copy-start(f32[862,20]{0,1:T(8,128)S(1)} %convolution_multiply_fusion) | copy-start | bytes 206884
  327.0 274.3 %all-gather.9.cloned.1.call-start = ((), (), s32[]{:S(2)}) async-start(), calls=%async_computation.1 | async-start | bytes 11096064 | tf_op jit(solution)/shard_map/all_gather | solution.py:14
  463.7 7.6 %copy-start.4 = (f32[20,862]{1,0:T(8,128)S(1)}, f32[20,862]{1,0:T(8,128)}, u32[]{:S(2)}) copy-start(f32[20,862]{1,0:T(8,128)} %reduce_sum.54) | copy-start | bytes 206884
  473.7 132.3 %copy-start.5 = (f32[20,862]{1,0:T(8,128)S(1)}, f32[20,862]{1,0:T(8,128)}, u32[]{:S(2)}) copy-start(f32[20,862]{1,0:T(8,128)} %reduce_sum.54) | copy-start | bytes 206884
  607.6 45.6 %copy-start.8 = (f32[20,862]{1,0:T(8,128)}, f32[20,862]{1,0:T(8,128)S(1)}, u32[]{:S(2)}) copy-start(f32[20,862]{1,0:T(8,128)S(1)} %get-tuple-element.57) | copy-start | bytes 206884
Sparse Core Ops, SparseCore 0:
  327.1 131.2 all-gather.6
  473.1 128.0 all-gather.8
where the time goes:
time: 667 us; the launch traced here: 660 us
  waiting for transfers between devices  259 us (39%)
  other arithmetic  252 us (38%)
  local copies, waits for them, and re-layouts  46.1 us (7%)
  blocking collectives  45.4 us (7%)
  matrix products  37.7 us (6%)
  between operations  20 us (3%)
    all_gather x2, waiting for transfers between devices, total_of_pieces(): tiles = lax.all_gather(array, axis)  259 us
    another operation x26, other arithmetic, shards(): jnp.linalg.cholesky(gram_matrix + penalty * jnp.eye(width, dtype=jnp.floa...  149 us
    another operation x8, other arithmetic, solve_rows(): return jax.scipy.linalg.cho_solve((factor, True), right_side.T).T  72.5 us
    psum x4, blocking collectives, by_axis(): array = lax.psum(array, axis)  40.7 us
    another operation x26, local copies, waits for them, and re-layouts, solve_rows(): return jax.scipy.linalg.cho_solve((factor, True), right_side.T).T  19.2 us
    another operation x12, matrix products, shards(): jnp.linalg.cholesky(gram_matrix + penalty * jnp.eye(width, dtype=jnp.floa...  13.7 us
  transfers between devices with their start and end apart: 2, of which 2 were waited for; matrix products, arithmetic and copies ran while one was open for 0% of the time, Pallas kernels for 0%

commit v1 on v0

--- a/solution.py
+++ b/solution.py
@@ -8,6 +8,12 @@
 SLAB = ("slab_0", "slab_1", "slab_2")
 SLAB_FEAT = ("slab_0", "slab_1", "slab_2", "feat")
 penalty = 1.0
+
+
+def play_vectors(x_local, comm_axis):
+    near = lax.all_gather(x_local, comm_axis)
+    q_next = jnp.sum(near, 0)
+    return q_next
 
 
 def total_of_pieces(array, axis):
@@ -31,7 +37,7 @@
 
 def by_axis(array, axes):
     for axis in axes:
-        array = lax.psum(array, axis)
+        array = play_vectors(array, axis)
     return array
 
 

time: 667 us -> 689 us (1.033)
  local copies, waits for them, and re-layouts: 46.1 us -> 70.8 us
    psum x4 -> x0, blocking collectives: 40.7 us -> none  [by_axis(): array = lax.psum(array, axis)]
    unnamed x0 -> x4, blocking collectives: none -> 37.9 us
    unnamed x46 -> x86, local copies, waits for them, and re-layouts: 7.24 us -> 34.4 us
    reduce_sum x0 -> x16, other arithmetic: none -> 9.77 us  [play_vectors(): q_next = jnp.sum(near, 0)]
  transfers between devices with their start and end apart: 2 -> 2, of which waited for: 2 -> 2; matrix products, arithmetic and copies ran while one was open for 0% -> 1% of each run, Pallas kernels for 0% -> 0%
where the time goes in v1:
time: 689 us; the launch traced here: 682 us
  other arithmetic  256 us (37%)
  waiting for transfers between devices  256 us (37%)
  local copies, waits for them, and re-layouts  70.8 us (10%)
  blocking collectives  42.6 us (6%)
  matrix products  36.1 us (5%)
  between operations  19.9 us (3%)
    all_gather x2, waiting for transfers between devices, total_of_pieces(): tiles = lax.all_gather(array, axis)  256 us
    another operation x26, other arithmetic, shards(): jnp.linalg.cholesky(gram_matrix + penalty * jnp.eye(width, dtype=jnp.floa...  145 us
    another operation x8, other arithmetic, solve_rows(): return jax.scipy.linalg.cho_solve((factor, True), right_side.T).T  72.2 us
    unnamed x4, blocking collectives  37.9 us
    unnamed x86, local copies, waits for them, and re-layouts  34.4 us
    another operation x26, local copies, waits for them, and re-layouts, solve_rows(): return jax.scipy.linalg.cho_solve((factor, True), right_side.T).T  18 us
  transfers between devices with their start and end apart: 2, of which 2 were waited for; matrix products, arithmetic and copies ran while one was open for 1% of the time, Pallas kernels for 0%

profile of v1, /device:TPU:1, one launch (start us, length us, event | category | flops | bytes accessed | tf_op | source)
XLA Modules:
  0.0 681.7 jit_solution(10247175323940923915)
XLA Ops:
  8.0 4.8 all_gather.111
  23.6 11.9 %concatenate.49 = f32[862,512]{1,0:T(8,128)S(1)} concatenate(f32[40,512]{1,0:T(8,128)S(1)} %get-tuple-element.61, f32[40,512]{1,0:T(8,128)S(1)} %broadcast_multiply_fusion.1, f32[39,512]{1,0:T(8,128)S(1)} %slice_multiply_fusion.6, f32[38,512]{1,0:T(8,128)S(1)} %slice_multiply_fusion.5, f32[37,512]{1,0:T(8,128)S(1)} %slice_multiply_fusion.4, f32[36,512]{1,0:T(8,128)S(1)} %slice_multiply_fusion.3, ...), dimensions={0} | concatenate | bytes 3530752 | tf_op jit(solution)/shard_map/concatenate | solution.py:51
  35.5 7.8 %convert_add_fusion = (f32[862,862]{0,1:T(8,128)}, f32[862,862]{0,1:T(8,128)}) fusion(f32[862,512]{1,0:T(8,128)S(1)} %concatenate.49), kind=kOutput, calls=%fused_computation.8 | convolution fusion | flops 4568234496 | bytes 7709728 | tf_op jit(solution)/shard_map/dot_general | solution.py:55
  43.3 3.9 copy.12
  51.1 11.7 %cholesky.196 = f32[128,128]{1,0:T(8,128)S(1)} custom-call(f32[128,128]{1,0:T(8,128)S(1)} %cholesky.508), custom_call_target="Cholesky" | custom-call | tf_op jit(solution)/shard_map/jit(cholesky)/cholesky | solution.py:79
  63.0 9.8 %custom-call.56 = f32[1,128,128]{1,2,0:T(8,128)S(1)} custom-call(f32[1,128,128]{2,1,0:T(8,128)S(1)} %get-tuple-element.118), custom_call_target="InvertDiagBlocksLowerTriangular" | custom-call | tf_op jit(solution)/shard_map/jit(cholesky)/cholesky | solution.py:79
  76.4 12.5 %cholesky.217 = f32[128,128]{1,0:T(8,128)S(1)} custom-call(f32[128,128]{1,0:T(8,128)} %cholesky.512), custom_call_target="Cholesky" | custom-call | tf_op jit(solution)/shard_map/jit(cholesky)/cholesky | solution.py:79
  89.6 10.8 %custom-call.57 = f32[1,128,128]{1,2,0:T(8,128)S(1)} custom-call(f32[1,128,128]{2,1,0:T(8,128)} %get-tuple-element.115), custom_call_target="InvertDiagBlocksLowerTriangular" | custom-call | tf_op jit(solution)/shard_map/jit(cholesky)/cholesky | solution.py:79
  102.5 11.7 %cholesky.413 = f32[128,128]{1,0:T(8,128)S(1)} custom-call(f32[128,128]{1,0:T(8,128)S(1)} %cholesky.517), custom_call_target="Cholesky" | custom-call | tf_op jit(solution)/shard_map/jit(cholesky)/cholesky | solution.py:79
  114.8 9.8 %custom-call.58 = f32[1,128,128]{1,2,0:T(8,128)S(1)} custom-call(f32[1,128,128]{2,1,0:T(8,128)S(1)} %get-tuple-element.112), custom_call_target="InvertDiagBlocksLowerTriangular" | custom-call | tf_op jit(solution)/shard_map/jit(cholesky)/cholesky | solution.py:79
  126.7 11.9 %cholesky.432 = f32[128,128]{1,0:T(8,128)S(1)} custom-call(f32[128,128]{1,0:T(8,128)S(1)} %cholesky.522), custom_call_target="Cholesky" | custom-call | tf_op jit(solution)/shard_map/jit(cholesky)/cholesky | solution.py:79
  139.4 9.8 %custom-call.59 = f32[1,128,128]{1,2,0:T(8,128)S(1)} custom-call(f32[1,128,128]{2,1,0:T(8,128)S(1)} %get-tuple-element.109), custom_call_target="InvertDiagBlocksLowerTriangular" | custom-call | tf_op jit(solution)/shard_map/jit(cholesky)/cholesky | solution.py:79
  151.2 11.7 %cholesky.451 = f32[128,128]{1,0:T(8,128)S(1)} custom-call(f32[128,128]{1,0:T(8,128)S(1)} %cholesky.527), custom_call_target="Cholesky" | custom-call | tf_op jit(solution)/shard_map/jit(cholesky)/cholesky | solution.py:79
  163.6 9.8 %custom-call.60 = f32[1,128,128]{1,2,0:T(8,128)S(1)} custom-call(f32[1,128,128]{2,1,0:T(8,128)S(1)} %get-tuple-element.106), custom_call_target="InvertDiagBlocksLowerTriangular" | custom-call | tf_op jit(solution)/shard_map/jit(cholesky)/cholesky | solution.py:79
  175.3 12.2 %cholesky.471 = f32[128,128]{1,0:T(8,128)S(1)} custom-call(f32[128,128]{1,0:T(8,128)S(1)} %cholesky.532), custom_call_target="Cholesky" | custom-call | tf_op jit(solution)/shard_map/jit(cholesky)/cholesky | solution.py:79
  188.1 9.8 %custom-call.61 = f32[1,128,128]{1,2,0:T(8,128)S(1)} custom-call(f32[1,128,128]{2,1,0:T(8,128)S(1)} %get-tuple-element.103), custom_call_target="InvertDiagBlocksLowerTriangular" | custom-call | tf_op jit(solution)/shard_map/jit(cholesky)/cholesky | solution.py:79
  199.3 8.6 %cholesky.492 = f32[94,94]{1,0:T(8,128)S(1)} custom-call(f32[94,94]{1,0:T(8,128)S(1)} %convolution_subtract_fusion.5), custom_call_target="Cholesky" | custom-call | tf_op jit(solution)/shard_map/jit(cholesky)/cholesky | solution.py:79
  215.6 17.4 %while.4 = (s32[]{:T(128)}, f32[862,862]{1,0:T(8,128)}, s32[6,2]{0,1:T(2,128)S(1)}, f32[6,128,128]{2,1,0:T(8,128)S(1)}, s32[]{:T(128)}) while((s32[]{:T(128)}, f32[862,862]{1,0:T(8,128)}, s32[6,2]{0,1:T(2,128)S(1)}, f32[6,128,128]{2,1,0:T(8,128)S(1)}, s32[]{:T(128)}) %tuple.121), condition=%wide.while_cond.clone, body=%wide.while_body.clone.sunk | while | flops 2 | bytes 131181 | solution.py:59
  216.2 2.3 bitcast_dynamic-update-slice_fusion.2
  219.1 2.3 bitcast_dynamic-update-slice_fusion.2
  222.0 2.3 bitcast_dynamic-update-slice_fusion.2
  224.9 2.3 bitcast_dynamic-update-slice_fusion.2
  234.0 69.9 %custom-call.64 = f32[7,128,128]{1,2,0:T(8,128)S(1)} custom-call(f32[7,128,128]{2,1,0:T(8,128)} %pad_maximum_fusion), custom_call_target="InvertDiagBlocksLowerTriangular" | custom-call | tf_op jit(solution)/shard_map/jit(_cho_solve)/triangular_solve | solution.py:59
  303.9 3.1 convolution_multiply_fusion
  317.9 131.3 %all-gather.7.cloned.1.call-done = f32[128,20,862]{2,1,0:T(8,128)} async-done(((f32[1,20,862]{2,1,0:T(8,128)}), f32[128,20,862]{2,1,0:T(8,128)}) %all-gather.7.cloned.1.call-update) | async-done | bytes 8826896 | tf_op jit(solution)/shard_map/all_gather | solution.py:20
  449.2 5.4 reduce_sum.198
  467.7 124.5 %all-gather.9.cloned.1.call-done = f32[128,20,862]{2,1,0:T(8,128)} async-done(((f32[1,20,862]{2,1,0:T(8,128)}), f32[128,20,862]{2,1,0:T(8,128)}) %all-gather.9.cloned.1.call-update) | async-done | bytes 8826896 | tf_op jit(solution)/shard_map/all_gather | solution.py:20
  592.1 4.8 reduce_sum.199
  604.7 11.7 %all-reduce.19 = (f32[8]{0:T(128)S(1)}, f32[8]{0:T(128)S(1)}, f32[8]{0:T(128)S(1)}, f32[8]{0:T(128)S(1)}) all-reduce(f32[8]{0:T(128)S(1)} %dynamic-update-slice.54, f32[8]{0:T(128)S(1)} %dynamic-update-slice.50, f32[8]{0:T(128)S(1)} %dynamic-update-slice.46, ...), channel_id=1, replica_groups=mesh['slab_0'=8,'slab_1'=4,'slab_2'=4,'feat'=2] {'slab_0'}, use_global_device_ids=true, to_apply=%add.15 | all-reduce | flops 32 | bytes 256
  624.8 8.4 %all-reduce.21 = (f32[4]{0:T(128)S(1)}, f32[4]{0:T(128)S(1)}, f32[4]{0:T(128)S(1)}, f32[4]{0:T(128)S(1)}) all-reduce(f32[4]{0:T(128)S(1)} %dynamic-update-slice.55, f32[4]{0:T(128)S(1)} %dynamic-update-slice.51, f32[4]{0:T(128)S(1)} %dynamic-update-slice.47, ...), channel_id=1, replica_groups=mesh['slab_0'=8,'slab_1'=4,'slab_2'=4,'feat'=2] {'slab_1'}, use_global_device_ids=true, to_apply=%add.16 | all-reduce | flops 16 | bytes 128
  642.0 6.6 all-reduce.20
  657.5 11.2 %all-reduce.22 = (f32[2]{0:T(128)S(1)}, f32[2]{0:T(128)S(1)}, f32[2]{0:T(128)S(1)}, f32[2]{0:T(128)S(1)}) all-reduce(f32[2]{0:T(128)S(1)} %dynamic-update-slice.57, f32[2]{0:T(128)S(1)} %dynamic-update-slice.53, f32[2]{0:T(128)S(1)} %dynamic-update-slice.49, ...), channel_id=1, replica_groups=mesh['slab_0'=8,'slab_1'=4,'slab_2'=4,'feat'=2] {'feat'}, use_global_device_ids=true, to_apply=%add.18 | all-reduce | flops 8 | bytes 64
  (273 shorter events, 107.2 us)
Async XLA Ops:
  7.2 442.0 %all-gather.7.cloned.1.call-start = ((), (), s32[]{:S(2)}) async-start(), calls=%async_computation | async-start | bytes 11096064 | tf_op jit(solution)/shard_map/all_gather | solution.py:20
  35.5 7.8 %copy-start = (f32[862,512]{1,0:T(8,128)}, f32[862,512]{1,0:T(8,128)S(1)}, u32[]{:S(2)}) copy-start(f32[862,512]{1,0:T(8,128)S(1)} %concatenate.49) | copy-start | bytes 5296132
  49.4 1.6 copy-start.3
  213.7 0.7 copy-start.11
  213.7 1.9 copy-start.7
  213.7 19.3 %copy-start.9 = (pred[34,34]{1,0:T(8,128)(4,1)S(1)}, pred[34,34]{1,0:T(8,128)(4,1)}, u32[]{:S(2)}) copy-start(pred[34,34]{1,0:T(8,128)(4,1)} %iota_compare_fusion.7) | copy-start | bytes 3472
  214.0 1.6 copy-start.1
  233.1 74.1 %copy-start.2 = (f32[862,862]{1,0:T(8,128)S(1)}, f32[862,862]{1,0:T(8,128)}, u32[]{:S(2)}) copy-start(f32[862,862]{1,0:T(8,128)} %get-tuple-element.215) | copy-start | bytes 8916532
  307.0 10.8 %copy-start.6 = (f32[862,20]{0,1:T(8,128)}, f32[862,20]{0,1:T(8,128)S(1)}, u32[]{:S(2)}) copy-start(f32[862,20]{0,1:T(8,128)S(1)} %convolution_multiply_fusion) | copy-start | bytes 206884
  317.8 274.3 %all-gather.9.cloned.1.call-start = ((), (), s32[]{:S(2)}) async-start(), calls=%async_computation.1 | async-start | bytes 11096064 | tf_op jit(solution)/shard_map/all_gather | solution.py:20
  454.6 7.6 %copy-start.4 = (f32[20,862]{1,0:T(8,128)S(1)}, f32[20,862]{1,0:T(8,128)}, u32[]{:S(2)}) copy-start(f32[20,862]{1,0:T(8,128)} %reduce_sum.198) | copy-start | bytes 206884
  467.6 129.2 %copy-start.5 = (f32[20,862]{1,0:T(8,128)S(1)}, f32[20,862]{1,0:T(8,128)}, u32[]{:S(2)}) copy-start(f32[20,862]{1,0:T(8,128)} %reduce_sum.198) | copy-start | bytes 206884
  467.7 136.4 %copy-start.10 = (u32[256]{0:T(256)S(1)}, u32[256]{0:T(256)}, u32[]{:S(2)}) copy-start(u32[256]{0:T(256)} %constant.325) | copy-start | bytes 3076
  598.5 76.1 %copy-start.8 = (f32[20,862]{1,0:T(8,128)}, f32[20,862]{1,0:T(8,128)S(1)}, u32[]{:S(2)}) copy-start(f32[20,862]{1,0:T(8,128)S(1)} %get-tuple-element.57) | copy-start | bytes 206884
Sparse Core Ops, SparseCore 0:
  317.9 131.2 all-gather.6
  463.9 128.1 all-gather.8
